TPU v7x, 128 devices: a whole 4x4x4 slice. The times are simulated.
128 devices in a mesh: freq: 2 (over core), dir: 4 (over y), ap: 16 (over z, x).
Axes of the slice: x: 4, y: 4, z: 4, core: 2. Of those that a mesh axis runs over, the one named last changes fastest.
Arguments:
- signal: bfloat16 [2, 65536, 2048], P(None, 'ap', ('freq', 'dir')), parts along dimension 2, may hold values from -6 to 6
- positions: int32 [2, 65536], P(None, 'ap'), may hold values from 0 to 255
- weights: bfloat16 [4, 2, 2, 2, 256, 256], replicated, may hold values from -0.1875 to 0.1875
- directions: int32 [2, 16, 4096], P(None, 'ap', 'dir'), may hold values from 0 to 255
Outputs:
- beams: bfloat16 [2, 16, 4096, 2048], P(None, 'ap', 'dir', 'freq'), parts along dimension 3
There are 2 independent parts, one for each index of `freq`. A program takes and returns all parts, laid end to end along the dimension named above; an argument that names none is the same for every part. Nothing has to cross between parts.
All inputs are finite; a program needn't handle non-finite values.
Results may differ from a plain program's by a relative error of at most 0.009.
Values may be sent and summed in bfloat16 or wider, within the bound.
No kernel may reach another device: no remote copies, remote signals or barrier semaphores. Data moves between devices by JAX's collectives and lax.ppermute only.
A program may use at most 128 MiB of HBM per device.

v0:
```python
import math

import jax
import jax.numpy as jnp
from jax import lax
from jax.experimental import pallas as pl
from jax.experimental.pallas import tpu as pltpu
from jax.sharding import Mesh, PartitionSpec as P


K = 256
EB = 256
SIDE = 16
BOXES = 16
COLS = 256
F32 = jnp.float32
BF = jnp.bfloat16


def sincos(phase):
    p = jnp.bitwise_and(phase, 255)
    q = jnp.right_shift(p + 32, 6)
    t = (p - jnp.left_shift(q, 6)).astype(F32) * (2.0 * math.pi / 256.0)
    u = t * t
    s0 = t * (1.0 + u * (-1.0 / 6 + u * (1.0 / 120 + u * (-1.0 / 5040 + u * (1.0 / 362880)))))
    c0 = 1.0 + u * (-0.5 + u * (1.0 / 24 + u * (-1.0 / 720 + u * (1.0 / 40320))))
    odd = jnp.bitwise_and(q, 1) == 1
    c = jnp.where(odd, s0, c0)
    s = jnp.where(odd, c0, s0)
    c = jnp.where(jnp.bitwise_and(q + 1, 2) == 2, -c, c)
    s = jnp.where(jnp.bitwise_and(q, 2) == 2, -s, s)
    return c, s


def dot(a, b):
    return jnp.dot(a, b, preferred_element_type=F32)


def place(offset):
    return jnp.where(offset == 0, 3, jnp.where(offset == 2, 0, jnp.where(offset == 1, 1, 2)))


def dft4(x):
    (a, b), (c, d), (e, f), (g, h) = x
    s0r, s0i, d0r, d0i = a + e, b + f, a - e, b - f
    s1r, s1i, d1r, d1i = c + g, d + h, c - g, d - h
    return (
        (s0r + s1r, s0i + s1i),
        (d0r + d1i, d0i - d1r),
        (s0r - s1r, s0i - s1i),
        (d0r - d1i, d0i + d1r),
    )


def expand_right(row_form):
    n = row_form.shape[-1] // 2
    r, i = row_form[:, :n], row_form[:, n:]
    return jnp.concatenate(
        [jnp.concatenate([r, i], 1), jnp.concatenate([-i, r], 1)], 0
    )


VMEM = pltpu.VMEM


def lead_kernel(pos_hbm, sig_hbm, w_hbm, *rest):
    outs, scratch = rest[:7], rest[7:]
    p2hi, p2lo, q1u, q1w, qmw, qmu, own = outs
    pos, sig, w, ax_c, ax_s, by_c, by_s, t0, t1, c0, d, mm, w43, e21, wsem, ssem = scratch
    core, own_z, own_x = (lax.axis_index(n) for n in ("freq", "z", "x"))
    child = (own_z // 2, own_z % 2, own_x // 2, own_x % 2)

    pos_copy = pltpu.make_async_copy(pos_hbm, pos, wsem.at[4])
    pos_copy.start()
    w_copies = [
        pltpu.make_async_copy(w_hbm.at[i, :, child[i]], w.at[i], wsem.at[i])
        for i in range(4)
    ]
    for i in (3, 2, 1, 0):
        w_copies[i].start()
    quarter = sig.shape[1] // 4
    s_copies = [
        pltpu.make_async_copy(
            sig_hbm.at[:, pl.ds(i * quarter, quarter), :],
            sig.at[:, pl.ds(i * quarter, quarter), :],
            ssem.at[i],
        )
        for i in range(4)
    ]
    for c in s_copies:
        c.start()

    pos_copy.wait()
    wave = lax.broadcasted_iota(jnp.int32, (SIDE, 1), 0) - SIDE // 2

    def factors(i, _):
        lanes = pl.ds(pl.multiple_of(i * 512, 512), 512)
        xc, xs = sincos(wave * pos[0:1, lanes])
        ax_c[:, lanes] = xc * (1.0 / 16.0)
        ax_s[:, lanes] = xs * (1.0 / 16.0)
        yc, ys = sincos(wave * pos[1:2, lanes])
        by_c[:, lanes] = yc
        by_s[:, lanes] = ys
        return 0

    lax.fori_loop(0, pos.shape[1] // 512, factors, 0)

    row = lax.broadcasted_iota(jnp.int32, (K, K), 0)
    col = lax.broadcasted_iota(jnp.int32, (K, K), 1)
    kx, ky = row // 64, row // 16 % 4
    hx, hy = row // 4 % 4, row % 4
    source = (hx * 4 + kx) * 16 + hy * 4 + ky
    pick = jnp.where(source == col, 1.0, 0.0).astype(BF)

    def row_form(level, r):
        return jnp.concatenate([w[level, r, 0], w[level, r, 1]], 1)

    w_copies[3].wait()
    upper = jnp.concatenate(
        [dot(pick, row_form(3, r)).astype(BF) for r in range(2)], 0
    )
    w_copies[2].wait()
    for r3 in range(2):
        w43[pl.ds(r3 * 512, 512), :] = dot(upper, expand_right(row_form(2, r3))).astype(BF)
    w_copies[1].wait()
    w_copies[0].wait()
    lower = jnp.concatenate([row_form(1, r) for r in range(2)], 0)
    for r1 in range(2):
        both = dot(lower, expand_right(row_form(0, r1))).astype(BF)
        for r2 in range(2):
            e21[r1 * 2 + r2] = expand_right(both[r2 * K : (r2 + 1) * K])

    first = core == 0

    def composite(z, _):
        rz = place(jnp.bitwise_and(z - own_z, 3))
        right = e21[z]
        for x in range(4):
            rx = place(jnp.bitwise_and(x - own_x, 3))
            slot = jnp.where(first, rz * 4 + rx, rx * 4 + rz)
            product = dot(w43[pl.ds(x * K, K), :], right).astype(BF)
            mm[:, slot] = product.reshape(16, 16, 512)
        return 0

    lax.fori_loop(0, 4, composite, 0)

    def build(table, m):
        start = pl.multiple_of(m * EB, EB)
        bc = by_c[:, pl.ds(start, EB)]
        bs = by_s[:, pl.ds(start, EB)]
        for wx in range(SIDE):
            ac = ax_c[wx : wx + 1, pl.ds(start, EB)]
            as_ = ax_s[wx : wx + 1, pl.ds(start, EB)]
            table[pl.ds(wx * 16, 16), 0:EB] = (ac * bc - as_ * bs).astype(BF)
            table[pl.ds(wx * 16, 16), EB : 2 * EB] = (as_ * bc + ac * bs).astype(BF)

    def multiply(table, m):
        start = pl.multiple_of(m * EB, EB)
        sr = sig[0, pl.ds(start, EB), :]
        si = sig[1, pl.ds(start, EB), :]
        right = jnp.concatenate(
            [jnp.concatenate([sr, si], 1), jnp.concatenate([si, -sr], 1)], 0
        )
        c0[m] = dot(table[...], right)

    build(t0, 0)
    for c in s_copies:
        c.wait()

    def leaf(i, _):
        m = i * 2
        build(t1, m + 1)
        multiply(t0, m)
        build(t0, jnp.minimum(m + 2, BOXES - 1))
        multiply(t1, m + 1)
        return 0

    lax.fori_loop(0, BOXES // 2, leaf, 0)

    def along_x(i, _):
        rows = pl.ds(pl.multiple_of(i * 8, 8), 8)
        for half in range(2):
            re_at, im_at = pl.ds(half * 128, 128), pl.ds(COLS + half * 128, 128)
            for my in range(4):
                x = [(c0[my * 4 + mx, rows, re_at], c0[my * 4 + mx, rows, im_at]) for mx in range(4)]
                for kx_, (re, im) in enumerate(dft4(x)):
                    c0[my * 4 + kx_, rows, re_at] = re
                    c0[my * 4 + kx_, rows, im_at] = im
        return 0

    lax.fori_loop(0, K // 8, along_x, 0)

    def along_y(i, _):
        rows = pl.ds(pl.multiple_of(i * 16, 16), 16)
        low = pl.ds(pl.multiple_of(i * 16 + K, 16), 16)
        for half in range(2):
            re_at, im_at = pl.ds(half * 128, 128), pl.ds(COLS + half * 128, 128)
            for kx_ in range(4):
                x = [(c0[my * 4 + kx_, rows, re_at], c0[my * 4 + kx_, rows, im_at]) for my in range(4)]
                for ky_, (re, im) in enumerate(dft4(x)):
                    re = (re * 0.25).astype(BF)
                    im = (im * 0.25).astype(BF)
                    cls = kx_ * 4 + ky_
                    d[cls, rows, re_at] = re
                    d[cls, rows, im_at] = im
                    d[cls, low, re_at] = -im
                    d[cls, low, im_at] = re
        return 0

    lax.fori_loop(0, K // 16, along_y, 0)

    def apply(cls, _):
        left = mm[cls].reshape(K, 2 * K)
        rows = pl.ds(pl.multiple_of(cls * 16, 16), 16)
        out = dot(left, d[cls]).astype(BF).reshape(4, 4, 16, 2 * COLS)
        p2hi[:, rows, :] = out[0, 0:2]
        p2lo[:, rows, :] = out[0, 2:4]
        q1u[:, rows, :] = out[1, 0:2]
        q1w[:, rows, :] = out[1, 2:4]
        qmw[:, rows, :] = out[2, 0:2]
        qmu[:, rows, :] = out[2, 2:4]
        own[:, rows, :] = out[3]
        return 0

    lax.fori_loop(0, 16, apply, 0)


def vm(n):
    return [pl.BlockSpec(memory_space=VMEM)] * n


def shaped(*dims, dtype=BF):
    return jax.ShapeDtypeStruct(dims, dtype)


def lead(positions, signal, weights):
    ne = positions.shape[1]
    hbm = pl.BlockSpec(memory_space=pltpu.HBM)
    return pl.pallas_call(
        lead_kernel,
        out_shape=[shaped(n, K, 2 * COLS) for n in (2, 2, 2, 2, 2, 2, 4)],
        in_specs=[hbm] * 3,
        out_specs=vm(7),
        scratch_shapes=[VMEM(positions.shape, jnp.int32), VMEM(signal.shape, BF), VMEM((4, 2, 2, K, K), BF)]
        + [VMEM((SIDE, ne), F32)] * 4
        + [VMEM((K, 2 * EB), BF)] * 2
        + [
            VMEM((BOXES, K, 2 * COLS), F32),
            VMEM((16, 2 * K, 2 * COLS), BF),
            VMEM((16, 16, 16, 2 * K), BF),
            VMEM((4 * K, 2 * K), BF),
            VMEM((4, 2 * K, 2 * K), BF),
            pltpu.SemaphoreType.DMA((5,)),
            pltpu.SemaphoreType.DMA((4,)),
        ],
        compiler_params=pltpu.CompilerParams(vmem_limit_bytes=48 << 20),
        cost_estimate=pl.CostEstimate(
            flops=8_000_000_000, transcendentals=0, bytes_accessed=12 << 20
        ),
        name="lead",
    )(positions, signal, weights)


def steer_kernel(pos, out, table):
    r = lax.broadcasted_iota(jnp.int32, (SIDE, 1), 0)
    n = pos.shape[-1]
    u, v = pos[0, 0:1, :], pos[1, 0:1, :]
    for kx in range(4):
        ac, as_ = sincos((r // 4 * 4 + kx - 8) * u)
        ac, as_ = ac * (1.0 / 16.0), as_ * (1.0 / 16.0)
        for ky in range(4):
            bc, bs = sincos((r % 4 * 4 + ky - 8) * v)
            rows = pl.ds((kx * 4 + ky) * 16, 16)
            table[rows, :] = ac * bc - as_ * bs
            table[pl.ds((kx * 4 + ky) * 16 + K, 16), :] = as_ * bc + ac * bs
    for i in range(n // 128):
        for j in range(2 * K // 128):
            block = table[pl.ds(j * 128, 128), pl.ds(i * 128, 128)]
            out[pl.ds(i * 128, 128), pl.ds(j * 128, 128)] = block.T.astype(BF)


def steer(directions):
    n = directions.shape[-1]
    return pl.pallas_call(
        steer_kernel,
        out_shape=shaped(n, 2 * K),
        in_specs=vm(1),
        out_specs=vm(1)[0],
        scratch_shapes=[VMEM((2 * K, n), F32)],
        cost_estimate=pl.CostEstimate(
            flops=1_500_000_000, transcendentals=0, bytes_accessed=1 << 20
        ),
        compiler_params=pltpu.CompilerParams(vmem_limit_bytes=16 << 20),
        name="steer",
    )(directions)


def added(*terms):
    total = terms[0].astype(F32)
    for t in terms[1:]:
        total = total + t.astype(F32)
    return total


def call(kernel, shapes, *args):
    return pl.pallas_call(
        kernel,
        out_shape=shapes,
        in_specs=vm(len(args)),
        out_specs=vm(len(shapes)),
        compiler_params=pltpu.CompilerParams(vmem_limit_bytes=24 << 20),
    )(*args)


def merge_kernel(mine, received, *outs):
    if len(outs) == 1:
        outs[0][...] = added(mine[...], received[...]).astype(BF)
    else:
        for i, o in enumerate(outs):
            o[...] = added(mine[i], received[i]).astype(BF)


def sum_far_kernel(own, g1, gm, lo, hi):
    s = added(own[0], g1[0], gm[...]).astype(BF)
    lo[...] = s[: K // 2]
    hi[...] = s[K // 2 :]


def sum_near_kernel(own, g1u, gmb, g1w, gmu, tlo, thi, u1, um, s0):
    h = K // 2
    one = added(own[1], g1u[1], gmb[...])
    u1[0:h] = (one[:h] + tlo[...].astype(F32)).astype(BF)
    u1[h:] = one[h:].astype(BF)
    other = added(own[2], g1w[0], gmu[0])
    um[0:h] = other[:h].astype(BF)
    um[h:] = (other[h:] + thi[...].astype(F32)).astype(BF)
    s0[...] = added(own[3], g1w[1], gmu[1])


def total_kernel(s0, v1, vm_, z):
    z[...] = added(s0[...], v1[...], vm_[...]).astype(BF)


def beam_kernel(offsets, table, *rest):
    parts = rest[: len(offsets)]
    out, buf, sem = rest[-3:]
    y = lax.axis_index("dir")
    n = table.shape[0] // 2
    copies = []
    for i, offset in enumerate(offsets):
        right = expand_right(parts[i][...])
        column = pl.multiple_of(jnp.bitwise_and(y + offset, 3) * COLS, COLS)
        for r in range(2):
            slot = len(copies) % 2
            if len(copies) >= 2:
                copies[-2].wait()
            b = dot(table[pl.ds(r * n, n), :], right).astype(BF)
            buf[slot, 0] = b[:, :COLS]
            buf[slot, 1] = b[:, COLS:]
            copies.append(
                pltpu.make_async_copy(
                    buf.at[slot],
                    out.at[:, 0, pl.ds(r * n, n), pl.ds(column, COLS)],
                    sem.at[slot],
                )
            )
            copies[-1].start()
    for c in copies[-2:]:
        c.wait()


def beams(offsets, table, parts, previous, shape):
    n = table.shape[0]
    hbm = pl.BlockSpec(memory_space=pltpu.HBM)
    extra = [] if previous is None else [previous]
    return pl.pallas_call(
        lambda *refs: beam_kernel(offsets, *refs),
        out_shape=jax.ShapeDtypeStruct(shape, BF),
        in_specs=vm(1 + len(parts)) + [hbm] * len(extra),
        out_specs=hbm,
        scratch_shapes=[
            VMEM((2, 2, n // 2, COLS), BF),
            pltpu.SemaphoreType.DMA((2,)),
        ],
        input_output_aliases={} if previous is None else {1 + len(parts): 0},
        cost_estimate=pl.CostEstimate(
            flops=2_000_000_000, transcendentals=0, bytes_accessed=1 << 20
        ),
        compiler_params=pltpu.CompilerParams(vmem_limit_bytes=24 << 20),
        name="beams",
    )(table, *parts, *extra)


def ring(step, first):
    pairs = []
    for z in range(4):
        for x in range(4):
            along_z = ((z + step) % 4) * 4 + x
            along_x = z * 4 + (x + step) % 4
            core0, core1 = (along_z, along_x) if first else (along_x, along_z)
            pairs.append((z * 4 + x, core0))
            pairs.append((16 + z * 4 + x, 16 + core1))
    return pairs


def local(signal, positions, weights, directions):
    along = ("freq", "z", "x")

    def major(a, step):
        return lax.ppermute(a, along, ring(step, True))

    def minor(a, step):
        return lax.ppermute(a, along, ring(step, False))

    def across(a, step):
        return lax.ppermute(a, "dir", [(i, (i + step) % 4) for i in range(4)])

    def compute():
        p2hi, p2lo, q1u, q1w, qmw, qmu, own = lead(positions, signal, weights)
        table = steer(directions)
        block = shaped(K, 2 * COLS)
        rhi, rlo = major(p2hi, -1), major(p2lo, 1)
        gmu, g1u = major(qmu, -1), major(q1u, 1)
        wma, wmb = call(merge_kernel, [block, block], qmw, rhi)
        (w1,) = call(merge_kernel, [shaped(2, K, 2 * COLS)], q1w, rlo)
        gma, g1w, gmb = major(wma, -1), major(w1, 1), major(wmb, -1)
        half = shaped(K // 2, 2 * COLS)
        lo, hi = call(sum_far_kernel, [half, half], own, g1u, gma)
        tlo, thi = minor(lo, 1), minor(hi, -1)
        u1, um, s0 = call(
            sum_near_kernel,
            [block, block, shaped(K, 2 * COLS, dtype=F32)],
            own, g1u, gmb, g1w, gmu, tlo, thi,
        )
        v1, v_m = minor(u1, 1), minor(um, -1)
        (zz,) = call(total_kernel, [block], s0, v1, v_m)
        y1, ym, y2 = across(zz, 1), across(zz, -1), across(zz, 2)
        shape = (2, 1, directions.shape[2], signal.shape[2] * 4)
        result = beams((0,), table, (zz,), None, shape)
        result = beams((3, 1), table, (y1, ym), result, shape)
        return beams((2,), table, (y2,), result, shape)

    return compute()


def solution(mesh):
    split = Mesh(mesh.devices.reshape(2, 4, 4, 4), ("freq", "dir", "z", "x"))
    ap = ("z", "x")
    in_specs = (P(None, ap, ("freq", "dir")), P(None, ap), P(), P(None, ap, "dir"))
    out_specs = P(None, ap, "dir", "freq")
    return jax.shard_map(
        local, mesh=split, in_specs=in_specs, out_specs=out_specs, check_vma=False
    )
```

profile of v0, /device:TPU:0, one launch (start us, length us, event | category | flops | bytes accessed | tf_op | source)
XLA Modules:
  0.0 71.7 jit_solution(6657796969607184858)
XLA Ops:
  0.0 0.8 %copy-done = s32[2,4096]{1,0:T(2,128)S(1)} copy-done((s32[2,4096]{1,0:T(2,128)S(1)}, s32[2,4096]{1,0:T(2,128)}, u32[]{:S(2)}) %copy-start) | copy-done | bytes 32792
  0.8 17.2 %lead.1 = (bf16[2,256,512]{2,1,0:T(8,128)(2,1)S(1)}, bf16[2,256,512]{2,1,0:T(8,128)(2,1)S(1)}, bf16[2,256,512]{2,1,0:T(8,128)(2,1)S(1)}, bf16[2,256,512]{2,1,0:T...) custom-call(s32[2,4096]{1,0:T(2,128)S(1)} %copy-done, ...), custom_call_target="tpu_custom_call" | custom-call | flops 8000000000 | bytes 12582912 | tf_op jit(solution)/shard_map/lead/pallas_call | solution.py:239
  18.0 2.1 %collective-permute-start.3 = (bf16[2,256,512]{2,1,0:T(8,128)(2,1)S(1)}, bf16[2,256,512]{2,1,0:T(8,128)(2,1)S(1)}, u32[]{:S(2)}, u32[]{:S(2)}) collective-permute-start(bf16[2,256,512]{2,1,0:T(8,128)(2,1)S(1)} %get-tuple-element.25), channel_id=1, source_target_pairs={{0,4},{64,65},{1,5},{65,66},{2,6},{66,67},{3,7},{67,64},{4,8},{68,... | collective-permute-start | bytes 1572872 | tf_op jit(solution)/shard_map/ppermute | solution.py:410
  20.1 2.2 %collective-permute-start.1 = (bf16[2,256,512]{2,1,0:T(8,128)(2,1)S(1)}, bf16[2,256,512]{2,1,0:T(8,128)(2,1)S(1)}, u32[]{:S(2)}, u32[]{:S(2)}) collective-permute-start(bf16[2,256,512]{2,1,0:T(8,128)(2,1)S(1)} %get-tuple-element.22), channel_id=1, source_target_pairs={{0,12},{64,67},{1,13},{65,64},{2,14},{66,65},{3,15},{67,66},{4,0},... | collective-permute-start | bytes 1572872 | tf_op jit(solution)/shard_map/ppermute | solution.py:410
  22.3 3.2 %collective-permute-start.5 = (bf16[2,256,512]{2,1,0:T(8,128)(2,1)S(1)}, bf16[2,256,512]{2,1,0:T(8,128)(2,1)S(1)}, u32[]{:S(2)}, u32[]{:S(2)}) collective-permute-start(bf16[2,256,512]{2,1,0:T(8,128)(2,1)S(1)} %get-tuple-element.26), channel_id=1, source_target_pairs={{0,12},{64,67},{1,13},{65,64},{2,14},{66,65},{3,15},{67,66},{4,0},... | collective-permute-start | bytes 1572872 | tf_op jit(solution)/shard_map/ppermute | solution.py:410
  25.5 3.8 %collective-permute-done.3.received = bf16[2,256,512]{2,1,0:T(8,128)(2,1)S(1)} collective-permute-done((bf16[2,256,512]{2,1,0:T(8,128)(2,1)S(1)}, bf16[2,256,512]{2,1,0:T(8,128)(2,1)S(1)}, u32[]{:S(2)}, u32[]{:S(2)}) %collective-permute-start.3) | collective-permute-done | bytes 524320 | tf_op jit(solution)/shard_map/ppermute | solution.py:410
  29.7 3.3 %collective-permute-start.6 = (bf16[256,512]{1,0:T(8,128)(2,1)S(1)}, bf16[256,512]{1,0:T(8,128)(2,1)S(1)}, u32[]{:S(2)}, u32[]{:S(2)}) collective-permute-start(bf16[256,512]{1,0:T(8,128)(2,1)S(1)} %get-tuple-element.27), channel_id=1, source_target_pairs={{0,12},{64,67},{1,13},{65,64},{2,14},{66,65},{3,15},{67,66},{4,0},... | collective-permute-start | bytes 786440 | tf_op jit(solution)/shard_map/ppermute | solution.py:410
  33.0 0.8 %collective-permute-start.2 = (bf16[256,512]{1,0:T(8,128)(2,1)S(1)}, bf16[256,512]{1,0:T(8,128)(2,1)S(1)}, u32[]{:S(2)}, u32[]{:S(2)}) collective-permute-start(bf16[256,512]{1,0:T(8,128)(2,1)S(1)} %get-tuple-element.23), channel_id=1, source_target_pairs={{0,12},{64,67},{1,13},{65,64},{2,14},{66,65},{3,15},{67,66},{4,0},... | collective-permute-start | bytes 786440 | tf_op jit(solution)/shard_map/ppermute | solution.py:410
  33.8 1.2 %collective-permute-done.g1.g1u = bf16[2,256,512]{2,1,0:T(8,128)(2,1)S(1)} collective-permute-done((bf16[2,256,512]{2,1,0:T(8,128)(2,1)S(1)}, bf16[2,256,512]{2,1,0:T(8,128)(2,1)S(1)}, u32[]{:S(2)}, u32[]{:S(2)}) %collective-permute-start) | collective-permute-done | bytes 524320 | tf_op jit(solution)/shard_map/ppermute | solution.py:410
  35.0 2.7 %collective-permute-done.6.gm = bf16[256,512]{1,0:T(8,128)(2,1)S(1)} collective-permute-done((bf16[256,512]{1,0:T(8,128)(2,1)S(1)}, bf16[256,512]{1,0:T(8,128)(2,1)S(1)}, u32[]{:S(2)}, u32[]{:S(2)}) %collective-permute-start.6) | collective-permute-done | bytes 262176 | tf_op jit(solution)/shard_map/ppermute | solution.py:410
  37.8 1.6 %collective-permute-start.7 = (bf16[128,512]{1,0:T(8,128)(2,1)S(1)}, bf16[128,512]{1,0:T(8,128)(2,1)S(1)}, u32[]{:S(2)}, u32[]{:S(2)}) collective-permute-start(bf16[128,512]{1,0:T(8,128)(2,1)S(1)} %get-tuple-element.28), channel_id=1, source_target_pairs={{0,1},{64,68},{1,2},{65,69},{2,3},{66,70},{3,0},{67,71},{4,5},{68,... | collective-permute-start | bytes 393224 | tf_op jit(solution)/shard_map/ppermute | solution.py:413
  39.4 1.8 %collective-permute-start.8 = (bf16[128,512]{1,0:T(8,128)(2,1)S(1)}, bf16[128,512]{1,0:T(8,128)(2,1)S(1)}, u32[]{:S(2)}, u32[]{:S(2)}) collective-permute-start(bf16[128,512]{1,0:T(8,128)(2,1)S(1)} %get-tuple-element.29), channel_id=1, source_target_pairs={{0,3},{64,76},{1,0},{65,77},{2,1},{66,78},{3,2},{67,79},{4,7},{68,... | collective-permute-start | bytes 393224 | tf_op jit(solution)/shard_map/ppermute | solution.py:413
  41.1 2.9 %collective-permute-done.7.tlo = bf16[128,512]{1,0:T(8,128)(2,1)S(1)} collective-permute-done((bf16[128,512]{1,0:T(8,128)(2,1)S(1)}, bf16[128,512]{1,0:T(8,128)(2,1)S(1)}, u32[]{:S(2)}, u32[]{:S(2)}) %collective-permute-start.7) | collective-permute-done | bytes 131104 | tf_op jit(solution)/shard_map/ppermute | solution.py:413
  44.6 1.6 %collective-permute-start.9 = (bf16[256,512]{1,0:T(8,128)(2,1)S(1)}, bf16[256,512]{1,0:T(8,128)(2,1)S(1)}, u32[]{:S(2)}, u32[]{:S(2)}) collective-permute-start(bf16[256,512]{1,0:T(8,128)(2,1)S(1)} %get-tuple-element.31), channel_id=1, source_target_pairs={{0,1},{64,68},{1,2},{65,69},{2,3},{66,70},{3,0},{67,71},{4,5},{68,... | collective-permute-start | bytes 786440 | tf_op jit(solution)/shard_map/ppermute | solution.py:413
  46.2 1.7 %collective-permute-start.10 = (bf16[256,512]{1,0:T(8,128)(2,1)S(1)}, bf16[256,512]{1,0:T(8,128)(2,1)S(1)}, u32[]{:S(2)}, u32[]{:S(2)}) collective-permute-start(bf16[256,512]{1,0:T(8,128)(2,1)S(1)} %get-tuple-element.32), channel_id=1, source_target_pairs={{0,3},{64,76},{1,0},{65,77},{2,1},{66,78},{3,2},{67,79},{4,7},{68,... | collective-permute-start | bytes 786440 | tf_op jit(solution)/shard_map/ppermute | solution.py:413
  47.9 4.3 %collective-permute-done.9.v1 = bf16[256,512]{1,0:T(8,128)(2,1)S(1)} collective-permute-done((bf16[256,512]{1,0:T(8,128)(2,1)S(1)}, bf16[256,512]{1,0:T(8,128)(2,1)S(1)}, u32[]{:S(2)}, u32[]{:S(2)}) %collective-permute-start.9) | collective-permute-done | bytes 262176 | tf_op jit(solution)/shard_map/ppermute | solution.py:413
  52.7 3.1 %collective-permute-start.13 = (bf16[256,512]{1,0:T(8,128)(2,1)S(1)}, bf16[256,512]{1,0:T(8,128)(2,1)S(1)}, u32[]{:S(2)}, u32[]{:S(2)}) collective-permute-start(bf16[256,512]{1,0:T(8,128)(2,1)S(1)} %shard_map.50.refs_1_), channel_id=1, source_target_pairs={{0,48},{16,0},{32,16},{48,32},{1,49},{17,1},{33,17},{49,33},{2,50}... | collective-permute-start | bytes 786440 | tf_op jit(solution)/shard_map/ppermute | solution.py:416
  55.7 1.2 %steer.1.refs_0_ = bf16[1024,512]{1,0:T(8,128)(2,1)S(1)} custom-call(s32[2,1,1024]{2,1,0:T(1,128)S(1)} %copy-done.1), custom_call_target="tpu_custom_call" | custom-call | flops 1500000000 | bytes 1048576 | tf_op jit(solution)/shard_map/steer/pallas_call | solution.py:284
  56.9 2.3 %collective-permute-start.11 = (bf16[256,512]{1,0:T(8,128)(2,1)S(1)}, bf16[256,512]{1,0:T(8,128)(2,1)S(1)}, u32[]{:S(2)}, u32[]{:S(2)}) collective-permute-start(bf16[256,512]{1,0:T(8,128)(2,1)S(1)} %shard_map.50.refs_1_), channel_id=1, source_target_pairs={{0,32},{16,48},{32,0},{48,16},{1,33},{17,49},{33,1},{49,17},{2,34}... | collective-permute-start | bytes 786440 | tf_op jit(solution)/shard_map/ppermute | solution.py:416
  59.2 1.7 %beams.3.refs_3_ = bf16[2,1,1024,1024]{3,2,1,0:T(8,128)(2,1)} custom-call(bf16[1024,512]{1,0:T(8,128)(2,1)S(1)} %steer.1.refs_0_, bf16[256,512]{1,0:T(8,128)(2,1)S(1)} %shard_map.50.refs_1_), custom_call_target="tpu_custom_call" | custom-call | flops 2000000000 | bytes 1048576 | tf_op jit(solution)/shard_map/beams/pallas_call | solution.py:376
  60.9 4.3 %collective-permute-done.13.refs_2_ = bf16[256,512]{1,0:T(8,128)(2,1)S(1)} collective-permute-done((bf16[256,512]{1,0:T(8,128)(2,1)S(1)}, bf16[256,512]{1,0:T(8,128)(2,1)S(1)}, u32[]{:S(2)}, u32[]{:S(2)}) %collective-permute-start.13) | collective-permute-done | bytes 262176 | tf_op jit(solution)/shard_map/ppermute | solution.py:416
  65.2 1.9 %collective-permute-done.12.refs_1_ = bf16[256,512]{1,0:T(8,128)(2,1)S(1)} collective-permute-done((bf16[256,512]{1,0:T(8,128)(2,1)S(1)}, bf16[256,512]{1,0:T(8,128)(2,1)S(1)}, u32[]{:S(2)}, u32[]{:S(2)}) %collective-permute-start.12) | collective-permute-done | bytes 262176 | tf_op jit(solution)/shard_map/ppermute | solution.py:416
  67.1 2.9 %beams.4.refs_2_ = bf16[2,1,1024,1024]{3,2,1,0:T(8,128)(2,1)} custom-call(bf16[1024,512]{1,0:T(8,128)(2,1)S(1)} %steer.1.refs_0_, bf16[256,512]{1,0:T(8,128)(2,1)S(1)} %collective-permute-done.12.refs_1_, bf16[256,512]{1,0:T(8,128)(2,1)S(1)} %collective-permute-done.13.refs_2_, bf16[2,1,1024,1024]{3,2,1,0:T(8,128)(2,1)} %beams.3.refs_3_), custom_call_target="tpu_custom_call", output_to_operand_aliasing={{}: (3, {})} | custom-call | flops 2000000000 | bytes 1048576 | tf_op jit(solution)/shard_map/beams/pallas_call | solution.py:376
  70.0 1.7 %beams.5 = bf16[2,1,1024,1024]{3,2,1,0:T(8,128)(2,1)} custom-call(bf16[1024,512]{1,0:T(8,128)(2,1)S(1)} %steer.1.refs_0_, bf16[256,512]{1,0:T(8,128)(2,1)S(1)} %collective-permute-done.11.refs_1_, bf16[2,1,1024,1024]{3,2,1,0:T(8,128)(2,1)} %beams.4.refs_2_), custom_call_target="tpu_custom_call", output_to_operand_aliasing={{}: (2, {})} | custom-call | flops 2000000000 | bytes 1048576 | tf_op jit(solution)/shard_map/beams/pallas_call | solution.py:376
  (18 shorter events, 1.4 us)
Async XLA Ops:
  0.0 0.8 %copy-start = (s32[2,4096]{1,0:T(2,128)S(1)}, s32[2,4096]{1,0:T(2,128)}, u32[]{:S(2)}) copy-start(s32[2,4096]{1,0:T(2,128)} %pos_hbm.1) | copy-start | bytes 98308
  18.0 11.4 %collective-permute-start.3 = (bf16[2,256,512]{2,1,0:T(8,128)(2,1)S(1)}, bf16[2,256,512]{2,1,0:T(8,128)(2,1)S(1)}, u32[]{:S(2)}, u32[]{:S(2)}) collective-permute-start(bf16[2,256,512]{2,1,0:T(8,128)(2,1)S(1)} %get-tuple-element.25), channel_id=1, source_target_pairs={{0,4},{64,65},{1,5},{65,66},{2,6},{66,67},{3,7},{67,64},{4,8},{68,... | collective-permute-start | bytes 1572872 | tf_op jit(solution)/shard_map/ppermute | solution.py:410
  20.1 9.5 %collective-permute-start.1 = (bf16[2,256,512]{2,1,0:T(8,128)(2,1)S(1)}, bf16[2,256,512]{2,1,0:T(8,128)(2,1)S(1)}, u32[]{:S(2)}, u32[]{:S(2)}) collective-permute-start(bf16[2,256,512]{2,1,0:T(8,128)(2,1)S(1)} %get-tuple-element.22), channel_id=1, source_target_pairs={{0,12},{64,67},{1,13},{65,64},{2,14},{66,65},{3,15},{67,66},{4,0},... | collective-permute-start | bytes 1572872 | tf_op jit(solution)/shard_map/ppermute | solution.py:410
  22.3 12.7 %collective-permute-start = (bf16[2,256,512]{2,1,0:T(8,128)(2,1)S(1)}, bf16[2,256,512]{2,1,0:T(8,128)(2,1)S(1)}, u32[]{:S(2)}, u32[]{:S(2)}) collective-permute-start(bf16[2,256,512]{2,1,0:T(8,128)(2,1)S(1)} %get-tuple-element.20), channel_id=1, source_target_pairs={{0,4},{64,65},{1,5},{65,66},{2,6},{66,67},{3,7},{67,64},{4,8},{68,... | collective-permute-start | bytes 1572872 | tf_op jit(solution)/shard_map/ppermute | solution.py:410
  22.3 18.8 %collective-permute-start.5 = (bf16[2,256,512]{2,1,0:T(8,128)(2,1)S(1)}, bf16[2,256,512]{2,1,0:T(8,128)(2,1)S(1)}, u32[]{:S(2)}, u32[]{:S(2)}) collective-permute-start(bf16[2,256,512]{2,1,0:T(8,128)(2,1)S(1)} %get-tuple-element.26), channel_id=1, source_target_pairs={{0,12},{64,67},{1,13},{65,64},{2,14},{66,65},{3,15},{67,66},{4,0},... | collective-permute-start | bytes 1572872 | tf_op jit(solution)/shard_map/ppermute | solution.py:410
  29.4 26.4 %copy-start.1 = (s32[2,1,1024]{2,1,0:T(1,128)S(1)}, s32[2,1,1024]{2,1,0:T(1,128)}, u32[]{:S(2)}) copy-start(s32[2,1,1024]{2,1,0:T(1,128)} %pos.1) | copy-start | bytes 24580
  29.5 14.8 %collective-permute-start.4 = (bf16[2,256,512]{2,1,0:T(8,128)(2,1)S(1)}, bf16[2,256,512]{2,1,0:T(8,128)(2,1)S(1)}, u32[]{:S(2)}, u32[]{:S(2)}) collective-permute-start(bf16[2,256,512]{2,1,0:T(8,128)(2,1)S(1)} %shard_map.47), channel_id=1, source_target_pairs={{0,4},{64,65},{1,5},{65,66},{2,6},{66,67},{3,7},{67,64},{4,8},{68,... | collective-permute-start | bytes 1572872 | tf_op jit(solution)/shard_map/ppermute | solution.py:410
  29.7 8.0 %collective-permute-start.6 = (bf16[256,512]{1,0:T(8,128)(2,1)S(1)}, bf16[256,512]{1,0:T(8,128)(2,1)S(1)}, u32[]{:S(2)}, u32[]{:S(2)}) collective-permute-start(bf16[256,512]{1,0:T(8,128)(2,1)S(1)} %get-tuple-element.27), channel_id=1, source_target_pairs={{0,12},{64,67},{1,13},{65,64},{2,14},{66,65},{3,15},{67,66},{4,0},... | collective-permute-start | bytes 786440 | tf_op jit(solution)/shard_map/ppermute | solution.py:410
  33.0 8.1 %collective-permute-start.2 = (bf16[256,512]{1,0:T(8,128)(2,1)S(1)}, bf16[256,512]{1,0:T(8,128)(2,1)S(1)}, u32[]{:S(2)}, u32[]{:S(2)}) collective-permute-start(bf16[256,512]{1,0:T(8,128)(2,1)S(1)} %get-tuple-element.23), channel_id=1, source_target_pairs={{0,12},{64,67},{1,13},{65,64},{2,14},{66,65},{3,15},{67,66},{4,0},... | collective-permute-start | bytes 786440 | tf_op jit(solution)/shard_map/ppermute | solution.py:410
  37.8 6.2 %collective-permute-start.7 = (bf16[128,512]{1,0:T(8,128)(2,1)S(1)}, bf16[128,512]{1,0:T(8,128)(2,1)S(1)}, u32[]{:S(2)}, u32[]{:S(2)}) collective-permute-start(bf16[128,512]{1,0:T(8,128)(2,1)S(1)} %get-tuple-element.28), channel_id=1, source_target_pairs={{0,1},{64,68},{1,2},{65,69},{2,3},{66,70},{3,0},{67,71},{4,5},{68,... | collective-permute-start | bytes 393224 | tf_op jit(solution)/shard_map/ppermute | solution.py:413
  39.4 5.0 %collective-permute-start.8 = (bf16[128,512]{1,0:T(8,128)(2,1)S(1)}, bf16[128,512]{1,0:T(8,128)(2,1)S(1)}, u32[]{:S(2)}, u32[]{:S(2)}) collective-permute-start(bf16[128,512]{1,0:T(8,128)(2,1)S(1)} %get-tuple-element.29), channel_id=1, source_target_pairs={{0,3},{64,76},{1,0},{65,77},{2,1},{66,78},{3,2},{67,79},{4,7},{68,... | collective-permute-start | bytes 393224 | tf_op jit(solution)/shard_map/ppermute | solution.py:413
  44.6 7.7 %collective-permute-start.9 = (bf16[256,512]{1,0:T(8,128)(2,1)S(1)}, bf16[256,512]{1,0:T(8,128)(2,1)S(1)}, u32[]{:S(2)}, u32[]{:S(2)}) collective-permute-start(bf16[256,512]{1,0:T(8,128)(2,1)S(1)} %get-tuple-element.31), channel_id=1, source_target_pairs={{0,1},{64,68},{1,2},{65,69},{2,3},{66,70},{3,0},{67,71},{4,5},{68,... | collective-permute-start | bytes 786440 | tf_op jit(solution)/shard_map/ppermute | solution.py:413
  46.2 6.4 %collective-permute-start.10 = (bf16[256,512]{1,0:T(8,128)(2,1)S(1)}, bf16[256,512]{1,0:T(8,128)(2,1)S(1)}, u32[]{:S(2)}, u32[]{:S(2)}) collective-permute-start(bf16[256,512]{1,0:T(8,128)(2,1)S(1)} %get-tuple-element.32), channel_id=1, source_target_pairs={{0,3},{64,76},{1,0},{65,77},{2,1},{66,78},{3,2},{67,79},{4,7},{68,... | collective-permute-start | bytes 786440 | tf_op jit(solution)/shard_map/ppermute | solution.py:413
  52.7 12.5 %collective-permute-start.13 = (bf16[256,512]{1,0:T(8,128)(2,1)S(1)}, bf16[256,512]{1,0:T(8,128)(2,1)S(1)}, u32[]{:S(2)}, u32[]{:S(2)}) collective-permute-start(bf16[256,512]{1,0:T(8,128)(2,1)S(1)} %shard_map.50.refs_1_), channel_id=1, source_target_pairs={{0,48},{16,0},{32,16},{48,32},{1,49},{17,1},{33,17},{49,33},{2,50}... | collective-permute-start | bytes 786440 | tf_op jit(solution)/shard_map/ppermute | solution.py:416
  55.7 11.3 %collective-permute-start.12 = (bf16[256,512]{1,0:T(8,128)(2,1)S(1)}, bf16[256,512]{1,0:T(8,128)(2,1)S(1)}, u32[]{:S(2)}, u32[]{:S(2)}) collective-permute-start(bf16[256,512]{1,0:T(8,128)(2,1)S(1)} %shard_map.50.refs_1_), channel_id=1, source_target_pairs={{0,16},{16,32},{32,48},{48,0},{1,17},{17,33},{33,49},{49,1},{2,18}... | collective-permute-start | bytes 786440 | tf_op jit(solution)/shard_map/ppermute | solution.py:416
  56.9 13.1 %collective-permute-start.11 = (bf16[256,512]{1,0:T(8,128)(2,1)S(1)}, bf16[256,512]{1,0:T(8,128)(2,1)S(1)}, u32[]{:S(2)}, u32[]{:S(2)}) collective-permute-start(bf16[256,512]{1,0:T(8,128)(2,1)S(1)} %shard_map.50.refs_1_), channel_id=1, source_target_pairs={{0,32},{16,48},{32,0},{48,16},{1,33},{17,49},{33,1},{49,17},{2,34}... | collective-permute-start | bytes 786440 | tf_op jit(solution)/shard_map/ppermute | solution.py:416
where the time goes:
time: 72.2 us; the launch traced here: 71.7 us
  Pallas kernels  25.4 us (35%)
  starting transfers between devices  23.7 us (33%)
  waiting for transfers between devices  21.8 us (30%)
  local copies, waits for them, and re-layouts  0.76 us (1%)
    pallas_call x1, Pallas kernels, lead(): pl.pallas_call(lead_kernel, out_shape=[shaped(n, K, 2 * COLS) for n in (2...  17.2 us
    ppermute x7, starting transfers between devices, major(): return lax.ppermute(a, along, ring(step, True))  11.7 us
    ppermute x4, waiting for transfers between devices, minor(): return lax.ppermute(a, along, ring(step, False))  7.83 us
    ppermute x7, waiting for transfers between devices, major(): return lax.ppermute(a, along, ring(step, True))  7.75 us
    ppermute x4, starting transfers between devices, minor(): return lax.ppermute(a, along, ring(step, False))  6.61 us
    pallas_call x3, Pallas kernels, beams(): pl.pallas_call(lambda *refs: beam_kernel(offsets, *refs), out_shape=jax.S...  6.24 us
    ppermute x3, waiting for transfers between devices, across(): return lax.ppermute(a, 'dir', [(i, (i + step) % 4) for i in range(4)])  6.23 us
    ppermute x3, starting transfers between devices, across(): return lax.ppermute(a, 'dir', [(i, (i + step) % 4) for i in range(4)])  5.37 us
  transfers between devices with their start and end apart: 14, of which 9 were waited for; matrix products, arithmetic and copies ran while one was open for 0% of the time, Pallas kernels for 8%

commit v1 on v0

--- a/solution.py
+++ b/solution.py
@@ -132,7 +132,7 @@
 
     first = core == 0
 
-    def composite(z, _):
+    for z in range(4):
         rz = place(jnp.bitwise_and(z - own_z, 3))
         right = e21[z]
         for x in range(4):
@@ -140,63 +140,48 @@
             slot = jnp.where(first, rz * 4 + rx, rx * 4 + rz)
             product = dot(w43[pl.ds(x * K, K), :], right).astype(BF)
             mm[:, slot] = product.reshape(16, 16, 512)
-        return 0
-
-    lax.fori_loop(0, 4, composite, 0)
 
     def build(table, m):
-        start = pl.multiple_of(m * EB, EB)
-        bc = by_c[:, pl.ds(start, EB)]
-        bs = by_s[:, pl.ds(start, EB)]
+        lanes = slice(m * EB, (m + 1) * EB)
+        bc, bs = by_c[:, lanes], by_s[:, lanes]
         for wx in range(SIDE):
-            ac = ax_c[wx : wx + 1, pl.ds(start, EB)]
-            as_ = ax_s[wx : wx + 1, pl.ds(start, EB)]
-            table[pl.ds(wx * 16, 16), 0:EB] = (ac * bc - as_ * bs).astype(BF)
-            table[pl.ds(wx * 16, 16), EB : 2 * EB] = (as_ * bc + ac * bs).astype(BF)
+            ac, as_ = ax_c[wx : wx + 1, lanes], ax_s[wx : wx + 1, lanes]
+            table[wx * 16 : wx * 16 + 16, 0:EB] = (ac * bc - as_ * bs).astype(BF)
+            table[wx * 16 : wx * 16 + 16, EB : 2 * EB] = (as_ * bc + ac * bs).astype(BF)
 
     def multiply(table, m):
-        start = pl.multiple_of(m * EB, EB)
-        sr = sig[0, pl.ds(start, EB), :]
-        si = sig[1, pl.ds(start, EB), :]
+        sr = sig[0, m * EB : (m + 1) * EB, :]
+        si = sig[1, m * EB : (m + 1) * EB, :]
         right = jnp.concatenate(
             [jnp.concatenate([sr, si], 1), jnp.concatenate([si, -sr], 1)], 0
         )
         c0[m] = dot(table[...], right)
 
-    build(t0, 0)
-    for c in s_copies:
-        c.wait()
-
-    def leaf(i, _):
-        m = i * 2
-        build(t1, m + 1)
-        multiply(t0, m)
-        build(t0, jnp.minimum(m + 2, BOXES - 1))
-        multiply(t1, m + 1)
-        return 0
-
-    lax.fori_loop(0, BOXES // 2, leaf, 0)
-
-    def along_x(i, _):
-        rows = pl.ds(pl.multiple_of(i * 8, 8), 8)
-        for half in range(2):
-            re_at, im_at = pl.ds(half * 128, 128), pl.ds(COLS + half * 128, 128)
-            for my in range(4):
-                x = [(c0[my * 4 + mx, rows, re_at], c0[my * 4 + mx, rows, im_at]) for mx in range(4)]
+    def along_x(my, part):
+        for i in range(part * 8, part * 8 + 8):
+            rows = slice(i * 8, i * 8 + 8)
+            for half in range(2):
+                re_at = slice(half * 128, half * 128 + 128)
+                im_at = slice(COLS + half * 128, COLS + half * 128 + 128)
+                x = [
+                    (c0[my * 4 + mx, rows, re_at], c0[my * 4 + mx, rows, im_at])
+                    for mx in range(4)
+                ]
                 for kx_, (re, im) in enumerate(dft4(x)):
                     c0[my * 4 + kx_, rows, re_at] = re
                     c0[my * 4 + kx_, rows, im_at] = im
-        return 0
-
-    lax.fori_loop(0, K // 8, along_x, 0)
-
-    def along_y(i, _):
-        rows = pl.ds(pl.multiple_of(i * 16, 16), 16)
-        low = pl.ds(pl.multiple_of(i * 16 + K, 16), 16)
-        for half in range(2):
-            re_at, im_at = pl.ds(half * 128, 128), pl.ds(COLS + half * 128, 128)
-            for kx_ in range(4):
-                x = [(c0[my * 4 + kx_, rows, re_at], c0[my * 4 + kx_, rows, im_at]) for my in range(4)]
+
+    def along_y(kx_, part):
+        for i in range(part * 4, part * 4 + 4):
+            rows = slice(i * 16, i * 16 + 16)
+            low = slice(K + i * 16, K + i * 16 + 16)
+            for half in range(2):
+                re_at = slice(half * 128, half * 128 + 128)
+                im_at = slice(COLS + half * 128, COLS + half * 128 + 128)
+                x = [
+                    (c0[my * 4 + kx_, rows, re_at], c0[my * 4 + kx_, rows, im_at])
+                    for my in range(4)
+                ]
                 for ky_, (re, im) in enumerate(dft4(x)):
                     re = (re * 0.25).astype(BF)
                     im = (im * 0.25).astype(BF)
@@ -205,13 +190,10 @@
                     d[cls, rows, im_at] = im
                     d[cls, low, re_at] = -im
                     d[cls, low, im_at] = re
-        return 0
-
-    lax.fori_loop(0, K // 16, along_y, 0)
-
-    def apply(cls, _):
+
+    def apply(cls):
         left = mm[cls].reshape(K, 2 * K)
-        rows = pl.ds(pl.multiple_of(cls * 16, 16), 16)
+        rows = slice(cls * 16, cls * 16 + 16)
         out = dot(left, d[cls]).astype(BF).reshape(4, 4, 16, 2 * COLS)
         p2hi[:, rows, :] = out[0, 0:2]
         p2lo[:, rows, :] = out[0, 2:4]
@@ -220,9 +202,25 @@
         qmw[:, rows, :] = out[2, 0:2]
         qmu[:, rows, :] = out[2, 2:4]
         own[:, rows, :] = out[3]
-        return 0
-
-    lax.fori_loop(0, 16, apply, 0)
+
+    tables = (t0, t1)
+    build(t0, 0)
+    for m in range(BOXES):
+        if m % 4 == 0:
+            s_copies[m // 4].wait()
+        if m + 1 < BOXES:
+            build(tables[(m + 1) % 2], m + 1)
+        multiply(tables[m % 2], m)
+        if m >= 4:
+            along_x(m // 4 - 1, m % 4)
+    for part in range(4):
+        along_x(3, part)
+    for part in range(4):
+        along_y(0, part)
+    for cls in range(16):
+        if cls < 12:
+            along_y(cls // 4 + 1, cls % 4)
+        apply(cls)
 
 
 def vm(n):

time: 72.2 us -> 67.8 us (0.939)
  Pallas kernels: 25.4 us -> 20.9 us
    pallas_call x1, Pallas kernels: 17.2 us -> 12.7 us  [lead(): pl.pallas_call(lead_kernel, out_shape=[shaped(n, K, 2 * COLS) for n in (2...]
  transfers between devices with their start and end apart: 14 -> 14, of which waited for: 9 -> 9; matrix products, arithmetic and copies ran while one was open for 0% -> 0% of each run, Pallas kernels for 8% -> 9%
where the time goes in v1:
time: 67.8 us; the launch traced here: 67.3 us
  starting transfers between devices  23.9 us (35%)
  waiting for transfers between devices  21.6 us (32%)
  Pallas kernels  20.9 us (31%)
  local copies, waits for them, and re-layouts  0.76 us (1%)
    pallas_call x1, Pallas kernels, lead(): pl.pallas_call(lead_kernel, out_shape=[shaped(n, K, 2 * COLS) for n in (2...  12.7 us
    ppermute x7, starting transfers between devices, major(): return lax.ppermute(a, along, ring(step, True))  11.9 us
    ppermute x4, waiting for transfers between devices, minor(): return lax.ppermute(a, along, ring(step, False))  7.84 us
    ppermute x7, waiting for transfers between devices, major(): return lax.ppermute(a, along, ring(step, True))  7.56 us
    ppermute x4, starting transfers between devices, minor(): return lax.ppermute(a, along, ring(step, False))  6.61 us
    pallas_call x3, Pallas kernels, beams(): pl.pallas_call(lambda *refs: beam_kernel(offsets, *refs), out_shape=jax.S...  6.24 us
    ppermute x3, waiting for transfers between devices, across(): return lax.ppermute(a, 'dir', [(i, (i + step) % 4) for i in range(4)])  6.22 us
    ppermute x3, starting transfers between devices, across(): return lax.ppermute(a, 'dir', [(i, (i + step) % 4) for i in range(4)])  5.37 us
  transfers between devices with their start and end apart: 14, of which 9 were waited for; matrix products, arithmetic and copies ran while one was open for 0% of the time, Pallas kernels for 9%

profile of v1, /device:TPU:0, one launch (start us, length us, event | category | flops | bytes accessed | tf_op | source)
XLA Modules:
  0.0 67.3 jit_solution(4065524959626159132)
XLA Ops:
  0.0 0.8 %copy-done = s32[2,4096]{1,0:T(2,128)S(1)} copy-done((s32[2,4096]{1,0:T(2,128)S(1)}, s32[2,4096]{1,0:T(2,128)}, u32[]{:S(2)}) %copy-start) | copy-done | bytes 32792
  0.8 12.7 %lead.1 = (bf16[2,256,512]{2,1,0:T(8,128)(2,1)S(1)}, bf16[2,256,512]{2,1,0:T(8,128)(2,1)S(1)}, bf16[2,256,512]{2,1,0:T(8,128)(2,1)S(1)}, bf16[2,256,512]{2,1,0:T...) custom-call(s32[2,4096]{1,0:T(2,128)S(1)} %copy-done, ...), custom_call_target="tpu_custom_call" | custom-call | flops 8000000000 | bytes 12582912 | tf_op jit(solution)/shard_map/lead/pallas_call | solution.py:237
  13.5 2.1 %collective-permute-start.3 = (bf16[2,256,512]{2,1,0:T(8,128)(2,1)S(1)}, bf16[2,256,512]{2,1,0:T(8,128)(2,1)S(1)}, u32[]{:S(2)}, u32[]{:S(2)}) collective-permute-start(bf16[2,256,512]{2,1,0:T(8,128)(2,1)S(1)} %get-tuple-element.25), channel_id=1, source_target_pairs={{0,4},{64,65},{1,5},{65,66},{2,6},{66,67},{3,7},{67,64},{4,8},{68,... | collective-permute-start | bytes 1572872 | tf_op jit(solution)/shard_map/ppermute | solution.py:408
  15.6 2.2 %collective-permute-start.1 = (bf16[2,256,512]{2,1,0:T(8,128)(2,1)S(1)}, bf16[2,256,512]{2,1,0:T(8,128)(2,1)S(1)}, u32[]{:S(2)}, u32[]{:S(2)}) collective-permute-start(bf16[2,256,512]{2,1,0:T(8,128)(2,1)S(1)} %get-tuple-element.22), channel_id=1, source_target_pairs={{0,12},{64,67},{1,13},{65,64},{2,14},{66,65},{3,15},{67,66},{4,0},... | collective-permute-start | bytes 1572872 | tf_op jit(solution)/shard_map/ppermute | solution.py:408
  17.8 3.2 %collective-permute-start.5 = (bf16[2,256,512]{2,1,0:T(8,128)(2,1)S(1)}, bf16[2,256,512]{2,1,0:T(8,128)(2,1)S(1)}, u32[]{:S(2)}, u32[]{:S(2)}) collective-permute-start(bf16[2,256,512]{2,1,0:T(8,128)(2,1)S(1)} %get-tuple-element.26), channel_id=1, source_target_pairs={{0,12},{64,67},{1,13},{65,64},{2,14},{66,65},{3,15},{67,66},{4,0},... | collective-permute-start | bytes 1572872 | tf_op jit(solution)/shard_map/ppermute | solution.py:408
  21.0 3.8 %collective-permute-done.3.received = bf16[2,256,512]{2,1,0:T(8,128)(2,1)S(1)} collective-permute-done((bf16[2,256,512]{2,1,0:T(8,128)(2,1)S(1)}, bf16[2,256,512]{2,1,0:T(8,128)(2,1)S(1)}, u32[]{:S(2)}, u32[]{:S(2)}) %collective-permute-start.3) | collective-permute-done | bytes 524320 | tf_op jit(solution)/shard_map/ppermute | solution.py:408
  25.4 3.3 %collective-permute-start.6 = (bf16[256,512]{1,0:T(8,128)(2,1)S(1)}, bf16[256,512]{1,0:T(8,128)(2,1)S(1)}, u32[]{:S(2)}, u32[]{:S(2)}) collective-permute-start(bf16[256,512]{1,0:T(8,128)(2,1)S(1)} %get-tuple-element.27), channel_id=1, source_target_pairs={{0,12},{64,67},{1,13},{65,64},{2,14},{66,65},{3,15},{67,66},{4,0},... | collective-permute-start | bytes 786440 | tf_op jit(solution)/shard_map/ppermute | solution.py:408
  28.7 0.8 %collective-permute-start.2 = (bf16[256,512]{1,0:T(8,128)(2,1)S(1)}, bf16[256,512]{1,0:T(8,128)(2,1)S(1)}, u32[]{:S(2)}, u32[]{:S(2)}) collective-permute-start(bf16[256,512]{1,0:T(8,128)(2,1)S(1)} %get-tuple-element.23), channel_id=1, source_target_pairs={{0,12},{64,67},{1,13},{65,64},{2,14},{66,65},{3,15},{67,66},{4,0},... | collective-permute-start | bytes 786440 | tf_op jit(solution)/shard_map/ppermute | solution.py:408
  29.5 1.0 %collective-permute-done.g1.g1u = bf16[2,256,512]{2,1,0:T(8,128)(2,1)S(1)} collective-permute-done((bf16[2,256,512]{2,1,0:T(8,128)(2,1)S(1)}, bf16[2,256,512]{2,1,0:T(8,128)(2,1)S(1)}, u32[]{:S(2)}, u32[]{:S(2)}) %collective-permute-start) | collective-permute-done | bytes 524320 | tf_op jit(solution)/shard_map/ppermute | solution.py:408
  30.5 2.7 %collective-permute-done.6.gm = bf16[256,512]{1,0:T(8,128)(2,1)S(1)} collective-permute-done((bf16[256,512]{1,0:T(8,128)(2,1)S(1)}, bf16[256,512]{1,0:T(8,128)(2,1)S(1)}, u32[]{:S(2)}, u32[]{:S(2)}) %collective-permute-start.6) | collective-permute-done | bytes 262176 | tf_op jit(solution)/shard_map/ppermute | solution.py:408
  33.3 1.6 %collective-permute-start.7 = (bf16[128,512]{1,0:T(8,128)(2,1)S(1)}, bf16[128,512]{1,0:T(8,128)(2,1)S(1)}, u32[]{:S(2)}, u32[]{:S(2)}) collective-permute-start(bf16[128,512]{1,0:T(8,128)(2,1)S(1)} %get-tuple-element.28), channel_id=1, source_target_pairs={{0,1},{64,68},{1,2},{65,69},{2,3},{66,70},{3,0},{67,71},{4,5},{68,... | collective-permute-start | bytes 393224 | tf_op jit(solution)/shard_map/ppermute | solution.py:411
  34.9 1.7 %collective-permute-start.8 = (bf16[128,512]{1,0:T(8,128)(2,1)S(1)}, bf16[128,512]{1,0:T(8,128)(2,1)S(1)}, u32[]{:S(2)}, u32[]{:S(2)}) collective-permute-start(bf16[128,512]{1,0:T(8,128)(2,1)S(1)} %get-tuple-element.29), channel_id=1, source_target_pairs={{0,3},{64,76},{1,0},{65,77},{2,1},{66,78},{3,2},{67,79},{4,7},{68,... | collective-permute-start | bytes 393224 | tf_op jit(solution)/shard_map/ppermute | solution.py:411
  36.6 2.9 %collective-permute-done.7.tlo = bf16[128,512]{1,0:T(8,128)(2,1)S(1)} collective-permute-done((bf16[128,512]{1,0:T(8,128)(2,1)S(1)}, bf16[128,512]{1,0:T(8,128)(2,1)S(1)}, u32[]{:S(2)}, u32[]{:S(2)}) %collective-permute-start.7) | collective-permute-done | bytes 131104 | tf_op jit(solution)/shard_map/ppermute | solution.py:411
  40.1 1.6 %collective-permute-start.9 = (bf16[256,512]{1,0:T(8,128)(2,1)S(1)}, bf16[256,512]{1,0:T(8,128)(2,1)S(1)}, u32[]{:S(2)}, u32[]{:S(2)}) collective-permute-start(bf16[256,512]{1,0:T(8,128)(2,1)S(1)} %get-tuple-element.31), channel_id=1, source_target_pairs={{0,1},{64,68},{1,2},{65,69},{2,3},{66,70},{3,0},{67,71},{4,5},{68,... | collective-permute-start | bytes 786440 | tf_op jit(solution)/shard_map/ppermute | solution.py:411
  41.7 1.7 %collective-permute-start.10 = (bf16[256,512]{1,0:T(8,128)(2,1)S(1)}, bf16[256,512]{1,0:T(8,128)(2,1)S(1)}, u32[]{:S(2)}, u32[]{:S(2)}) collective-permute-start(bf16[256,512]{1,0:T(8,128)(2,1)S(1)} %get-tuple-element.32), channel_id=1, source_target_pairs={{0,3},{64,76},{1,0},{65,77},{2,1},{66,78},{3,2},{67,79},{4,7},{68,... | collective-permute-start | bytes 786440 | tf_op jit(solution)/shard_map/ppermute | solution.py:411
  43.4 4.3 %collective-permute-done.9.v1 = bf16[256,512]{1,0:T(8,128)(2,1)S(1)} collective-permute-done((bf16[256,512]{1,0:T(8,128)(2,1)S(1)}, bf16[256,512]{1,0:T(8,128)(2,1)S(1)}, u32[]{:S(2)}, u32[]{:S(2)}) %collective-permute-start.9) | collective-permute-done | bytes 262176 | tf_op jit(solution)/shard_map/ppermute | solution.py:411
  48.1 3.1 %collective-permute-start.13 = (bf16[256,512]{1,0:T(8,128)(2,1)S(1)}, bf16[256,512]{1,0:T(8,128)(2,1)S(1)}, u32[]{:S(2)}, u32[]{:S(2)}) collective-permute-start(bf16[256,512]{1,0:T(8,128)(2,1)S(1)} %shard_map.50.refs_1_), channel_id=1, source_target_pairs={{0,48},{16,0},{32,16},{48,32},{1,49},{17,1},{33,17},{49,33},{2,50}... | collective-permute-start | bytes 786440 | tf_op jit(solution)/shard_map/ppermute | solution.py:414
  51.2 1.2 %steer.1.refs_0_ = bf16[1024,512]{1,0:T(8,128)(2,1)S(1)} custom-call(s32[2,1,1024]{2,1,0:T(1,128)S(1)} %copy-done.1), custom_call_target="tpu_custom_call" | custom-call | flops 1500000000 | bytes 1048576 | tf_op jit(solution)/shard_map/steer/pallas_call | solution.py:282
  52.4 2.3 %collective-permute-start.11 = (bf16[256,512]{1,0:T(8,128)(2,1)S(1)}, bf16[256,512]{1,0:T(8,128)(2,1)S(1)}, u32[]{:S(2)}, u32[]{:S(2)}) collective-permute-start(bf16[256,512]{1,0:T(8,128)(2,1)S(1)} %shard_map.50.refs_1_), channel_id=1, source_target_pairs={{0,32},{16,48},{32,0},{48,16},{1,33},{17,49},{33,1},{49,17},{2,34}... | collective-permute-start | bytes 786440 | tf_op jit(solution)/shard_map/ppermute | solution.py:414
  54.7 1.7 %beams.3.refs_3_ = bf16[2,1,1024,1024]{3,2,1,0:T(8,128)(2,1)} custom-call(bf16[1024,512]{1,0:T(8,128)(2,1)S(1)} %steer.1.refs_0_, bf16[256,512]{1,0:T(8,128)(2,1)S(1)} %shard_map.50.refs_1_), custom_call_target="tpu_custom_call" | custom-call | flops 2000000000 | bytes 1048576 | tf_op jit(solution)/shard_map/beams/pallas_call | solution.py:374
  56.4 4.3 %collective-permute-done.13.refs_2_ = bf16[256,512]{1,0:T(8,128)(2,1)S(1)} collective-permute-done((bf16[256,512]{1,0:T(8,128)(2,1)S(1)}, bf16[256,512]{1,0:T(8,128)(2,1)S(1)}, u32[]{:S(2)}, u32[]{:S(2)}) %collective-permute-start.13) | collective-permute-done | bytes 262176 | tf_op jit(solution)/shard_map/ppermute | solution.py:414
  60.7 1.9 %collective-permute-done.12.refs_1_ = bf16[256,512]{1,0:T(8,128)(2,1)S(1)} collective-permute-done((bf16[256,512]{1,0:T(8,128)(2,1)S(1)}, bf16[256,512]{1,0:T(8,128)(2,1)S(1)}, u32[]{:S(2)}, u32[]{:S(2)}) %collective-permute-start.12) | collective-permute-done | bytes 262176 | tf_op jit(solution)/shard_map/ppermute | solution.py:414
  62.6 2.9 %beams.4.refs_2_ = bf16[2,1,1024,1024]{3,2,1,0:T(8,128)(2,1)} custom-call(bf16[1024,512]{1,0:T(8,128)(2,1)S(1)} %steer.1.refs_0_, bf16[256,512]{1,0:T(8,128)(2,1)S(1)} %collective-permute-done.12.refs_1_, bf16[256,512]{1,0:T(8,128)(2,1)S(1)} %collective-permute-done.13.refs_2_, bf16[2,1,1024,1024]{3,2,1,0:T(8,128)(2,1)} %beams.3.refs_3_), custom_call_target="tpu_custom_call", output_to_operand_aliasing={{}: (3, {})} | custom-call | flops 2000000000 | bytes 1048576 | tf_op jit(solution)/shard_map/beams/pallas_call | solution.py:374
  65.5 1.7 %beams.5 = bf16[2,1,1024,1024]{3,2,1,0:T(8,128)(2,1)} custom-call(bf16[1024,512]{1,0:T(8,128)(2,1)S(1)} %steer.1.refs_0_, bf16[256,512]{1,0:T(8,128)(2,1)S(1)} %collective-permute-done.11.refs_1_, bf16[2,1,1024,1024]{3,2,1,0:T(8,128)(2,1)} %beams.4.refs_2_), custom_call_target="tpu_custom_call", output_to_operand_aliasing={{}: (2, {})} | custom-call | flops 2000000000 | bytes 1048576 | tf_op jit(solution)/shard_map/beams/pallas_call | solution.py:374
  (18 shorter events, 1.6 us)
Async XLA Ops:
  0.0 0.8 %copy-start = (s32[2,4096]{1,0:T(2,128)S(1)}, s32[2,4096]{1,0:T(2,128)}, u32[]{:S(2)}) copy-start(s32[2,4096]{1,0:T(2,128)} %pos_hbm.1) | copy-start | bytes 98308
  13.5 11.4 %collective-permute-start.3 = (bf16[2,256,512]{2,1,0:T(8,128)(2,1)S(1)}, bf16[2,256,512]{2,1,0:T(8,128)(2,1)S(1)}, u32[]{:S(2)}, u32[]{:S(2)}) collective-permute-start(bf16[2,256,512]{2,1,0:T(8,128)(2,1)S(1)} %get-tuple-element.25), channel_id=1, source_target_pairs={{0,4},{64,65},{1,5},{65,66},{2,6},{66,67},{3,7},{67,64},{4,8},{68,... | collective-permute-start | bytes 1572872 | tf_op jit(solution)/shard_map/ppermute | solution.py:408
  15.6 9.7 %collective-permute-start.1 = (bf16[2,256,512]{2,1,0:T(8,128)(2,1)S(1)}, bf16[2,256,512]{2,1,0:T(8,128)(2,1)S(1)}, u32[]{:S(2)}, u32[]{:S(2)}) collective-permute-start(bf16[2,256,512]{2,1,0:T(8,128)(2,1)S(1)} %get-tuple-element.22), channel_id=1, source_target_pairs={{0,12},{64,67},{1,13},{65,64},{2,14},{66,65},{3,15},{67,66},{4,0},... | collective-permute-start | bytes 1572872 | tf_op jit(solution)/shard_map/ppermute | solution.py:408
  17.8 12.7 %collective-permute-start = (bf16[2,256,512]{2,1,0:T(8,128)(2,1)S(1)}, bf16[2,256,512]{2,1,0:T(8,128)(2,1)S(1)}, u32[]{:S(2)}, u32[]{:S(2)}) collective-permute-start(bf16[2,256,512]{2,1,0:T(8,128)(2,1)S(1)} %get-tuple-element.20), channel_id=1, source_target_pairs={{0,4},{64,65},{1,5},{65,66},{2,6},{66,67},{3,7},{67,64},{4,8},{68,... | collective-permute-start | bytes 1572872 | tf_op jit(solution)/shard_map/ppermute | solution.py:408
  17.8 18.8 %collective-permute-start.5 = (bf16[2,256,512]{2,1,0:T(8,128)(2,1)S(1)}, bf16[2,256,512]{2,1,0:T(8,128)(2,1)S(1)}, u32[]{:S(2)}, u32[]{:S(2)}) collective-permute-start(bf16[2,256,512]{2,1,0:T(8,128)(2,1)S(1)} %get-tuple-element.26), channel_id=1, source_target_pairs={{0,12},{64,67},{1,13},{65,64},{2,14},{66,65},{3,15},{67,66},{4,0},... | collective-permute-start | bytes 1572872 | tf_op jit(solution)/shard_map/ppermute | solution.py:408
  24.9 26.4 %copy-start.1 = (s32[2,1,1024]{2,1,0:T(1,128)S(1)}, s32[2,1,1024]{2,1,0:T(1,128)}, u32[]{:S(2)}) copy-start(s32[2,1,1024]{2,1,0:T(1,128)} %pos.1) | copy-start | bytes 24580
  25.0 14.8 %collective-permute-start.4 = (bf16[2,256,512]{2,1,0:T(8,128)(2,1)S(1)}, bf16[2,256,512]{2,1,0:T(8,128)(2,1)S(1)}, u32[]{:S(2)}, u32[]{:S(2)}) collective-permute-start(bf16[2,256,512]{2,1,0:T(8,128)(2,1)S(1)} %shard_map.47), channel_id=1, source_target_pairs={{0,4},{64,65},{1,5},{65,66},{2,6},{66,67},{3,7},{67,64},{4,8},{68,... | collective-permute-start | bytes 1572872 | tf_op jit(solution)/shard_map/ppermute | solution.py:408
  25.4 7.8 %collective-permute-start.6 = (bf16[256,512]{1,0:T(8,128)(2,1)S(1)}, bf16[256,512]{1,0:T(8,128)(2,1)S(1)}, u32[]{:S(2)}, u32[]{:S(2)}) collective-permute-start(bf16[256,512]{1,0:T(8,128)(2,1)S(1)} %get-tuple-element.27), channel_id=1, source_target_pairs={{0,12},{64,67},{1,13},{65,64},{2,14},{66,65},{3,15},{67,66},{4,0},... | collective-permute-start | bytes 786440 | tf_op jit(solution)/shard_map/ppermute | solution.py:408
  28.7 7.9 %collective-permute-start.2 = (bf16[256,512]{1,0:T(8,128)(2,1)S(1)}, bf16[256,512]{1,0:T(8,128)(2,1)S(1)}, u32[]{:S(2)}, u32[]{:S(2)}) collective-permute-start(bf16[256,512]{1,0:T(8,128)(2,1)S(1)} %get-tuple-element.23), channel_id=1, source_target_pairs={{0,12},{64,67},{1,13},{65,64},{2,14},{66,65},{3,15},{67,66},{4,0},... | collective-permute-start | bytes 786440 | tf_op jit(solution)/shard_map/ppermute | solution.py:408
  33.3 6.2 %collective-permute-start.7 = (bf16[128,512]{1,0:T(8,128)(2,1)S(1)}, bf16[128,512]{1,0:T(8,128)(2,1)S(1)}, u32[]{:S(2)}, u32[]{:S(2)}) collective-permute-start(bf16[128,512]{1,0:T(8,128)(2,1)S(1)} %get-tuple-element.28), channel_id=1, source_target_pairs={{0,1},{64,68},{1,2},{65,69},{2,3},{66,70},{3,0},{67,71},{4,5},{68,... | collective-permute-start | bytes 393224 | tf_op jit(solution)/shard_map/ppermute | solution.py:411
  34.9 5.0 %collective-permute-start.8 = (bf16[128,512]{1,0:T(8,128)(2,1)S(1)}, bf16[128,512]{1,0:T(8,128)(2,1)S(1)}, u32[]{:S(2)}, u32[]{:S(2)}) collective-permute-start(bf16[128,512]{1,0:T(8,128)(2,1)S(1)} %get-tuple-element.29), channel_id=1, source_target_pairs={{0,3},{64,76},{1,0},{65,77},{2,1},{66,78},{3,2},{67,79},{4,7},{68,... | collective-permute-start | bytes 393224 | tf_op jit(solution)/shard_map/ppermute | solution.py:411
  40.1 7.7 %collective-permute-start.9 = (bf16[256,512]{1,0:T(8,128)(2,1)S(1)}, bf16[256,512]{1,0:T(8,128)(2,1)S(1)}, u32[]{:S(2)}, u32[]{:S(2)}) collective-permute-start(bf16[256,512]{1,0:T(8,128)(2,1)S(1)} %get-tuple-element.31), channel_id=1, source_target_pairs={{0,1},{64,68},{1,2},{65,69},{2,3},{66,70},{3,0},{67,71},{4,5},{68,... | collective-permute-start | bytes 786440 | tf_op jit(solution)/shard_map/ppermute | solution.py:411
  41.7 6.4 %collective-permute-start.10 = (bf16[256,512]{1,0:T(8,128)(2,1)S(1)}, bf16[256,512]{1,0:T(8,128)(2,1)S(1)}, u32[]{:S(2)}, u32[]{:S(2)}) collective-permute-start(bf16[256,512]{1,0:T(8,128)(2,1)S(1)} %get-tuple-element.32), channel_id=1, source_target_pairs={{0,3},{64,76},{1,0},{65,77},{2,1},{66,78},{3,2},{67,79},{4,7},{68,... | collective-permute-start | bytes 786440 | tf_op jit(solution)/shard_map/ppermute | solution.py:411
  48.1 12.5 %collective-permute-start.13 = (bf16[256,512]{1,0:T(8,128)(2,1)S(1)}, bf16[256,512]{1,0:T(8,128)(2,1)S(1)}, u32[]{:S(2)}, u32[]{:S(2)}) collective-permute-start(bf16[256,512]{1,0:T(8,128)(2,1)S(1)} %shard_map.50.refs_1_), channel_id=1, source_target_pairs={{0,48},{16,0},{32,16},{48,32},{1,49},{17,1},{33,17},{49,33},{2,50}... | collective-permute-start | bytes 786440 | tf_op jit(solution)/shard_map/ppermute | solution.py:414
  51.2 11.3 %collective-permute-start.12 = (bf16[256,512]{1,0:T(8,128)(2,1)S(1)}, bf16[256,512]{1,0:T(8,128)(2,1)S(1)}, u32[]{:S(2)}, u32[]{:S(2)}) collective-permute-start(bf16[256,512]{1,0:T(8,128)(2,1)S(1)} %shard_map.50.refs_1_), channel_id=1, source_target_pairs={{0,16},{16,32},{32,48},{48,0},{1,17},{17,33},{33,49},{49,1},{2,18}... | collective-permute-start | bytes 786440 | tf_op jit(solution)/shard_map/ppermute | solution.py:414
  52.4 13.1 %collective-permute-start.11 = (bf16[256,512]{1,0:T(8,128)(2,1)S(1)}, bf16[256,512]{1,0:T(8,128)(2,1)S(1)}, u32[]{:S(2)}, u32[]{:S(2)}) collective-permute-start(bf16[256,512]{1,0:T(8,128)(2,1)S(1)} %shard_map.50.refs_1_), channel_id=1, source_target_pairs={{0,32},{16,48},{32,0},{48,16},{1,33},{17,49},{33,1},{49,17},{2,34}... | collective-permute-start | bytes 786440 | tf_op jit(solution)/shard_map/ppermute | solution.py:414
